TPU v7x, 32 devices: a whole 2x2x4 slice. The times are simulated.
32 devices in a mesh: blk: 4 (over y, x), grp: 8 (over z, core).
Axes of the slice: x: 2, y: 2, z: 4, core: 2. Of those that a mesh axis runs over, the one named last changes fastest.
Arguments:
- b3c: bfloat16 [384, 3, 32, 4096], P('blk', None, None, 'grp'), may hold values from -6 to 6
- green_occ: bfloat16 [384, 384], P('blk', 'grp'), may hold values from -0.3125 to 0.3125
- green_virt: bfloat16 [384, 384], P(None, 'grp'), may hold values from -0.625 to 0.625
- occ_mask: int32 [12, 12], replicated, may hold values from 0 to 1, as said below
- a_tiles: bfloat16 [128, 32, 1024], P(('blk', 'grp')), may hold values from -0.046875 to 0.046875
- tile_codes: int32 [128], P(('blk', 'grp')), may hold values from -1 to 143, as said below
Outputs:
- chi: float32 [512, 4096], P('blk', 'grp')
Inputs may be any that keep to these rules, and one draw needn't show every extreme that they name: `occ_mask`: the diagonal is 1. `tile_codes`: each device's 4 slots hold its live tiles first and -1 after them; some device has all 4 slots live; codes may repeat, and repeated tiles add.
All inputs are finite; a program needn't handle non-finite values.
Results may differ from a plain program's by a relative error of at most 0.0041.
Values may be sent and summed in bfloat16 or wider, within the bound.
No kernel may reach another device: no remote copies, remote signals or barrier semaphores. Data moves between devices by JAX's collectives and lax.ppermute only.
A program may use at most 192 MiB of HBM per device.

v0:
```python
import jax
import jax.numpy as jnp
from jax import lax
from jax.sharding import PartitionSpec as P

BS = 32
PB = 32
KB = 3
BAND = 3
PBD = 4


def local(b3c, green_occ, green_virt, occ_mask, a_tiles, tile_codes):
    group = lax.axis_index("blk")
    occ_all, virt_all = (
        lax.all_gather(green_occ, "grp", axis=1, tiled=True),
        lax.all_gather(green_virt, "grp", axis=1, tiled=True),
    )
    basis_total = virt_all.shape[1]
    block_total = basis_total // BS
    window = (KB + BAND - 1) * BS
    pair_count = KB * BAND
    query_local = b3c.shape[3]
    mask_rows = lax.dynamic_slice_in_dim(occ_mask, group * KB, KB, 0)
    mask_full = jnp.repeat(jnp.repeat(mask_rows, BS, axis=0), BS, axis=1).astype(jnp.bfloat16)
    occ_group = occ_all * mask_full
    rows = (group * KB * BS + jnp.arange(window, dtype=jnp.int32)) % basis_total
    virt_window = jnp.take(virt_all, rows, axis=0).reshape(window, block_total, BS)
    accumulate_piece = lax.all_gather(b3c, "blk", axis=0, tiled=True)
    count = accumulate_piece.shape[0]
    blocks_in = count // BS
    lam_index = jnp.arange(count, dtype=jnp.int32) % basis_total
    occ_cols = jnp.take(occ_group, lam_index, axis=1)
    lam_blocks = jnp.arange(blocks_in, dtype=jnp.int32) % block_total
    partner = (lam_blocks[:, None] + jnp.arange(BAND, dtype=jnp.int32)[None, :]) % block_total
    virt_sel = jnp.take(virt_window, partner, axis=1)
    tensor = accumulate_piece.reshape(blocks_in, BS, BAND, BS, query_local)
    inner = jnp.einsum("wlds,ladsq->lawq", virt_sel, tensor, preferred_element_type=jnp.float32)
    inner = inner.astype(jnp.bfloat16).reshape(count, window * query_local)
    paired = jnp.dot(occ_cols, inner, preferred_element_type=jnp.float32)
    paired = paired.reshape(KB * BS, window, query_local).astype(jnp.bfloat16)
    pieces = []
    for block in range(KB):
        for offset in range(BAND):
            piece = paired[
                block * BS : (block + 1) * BS, (block + offset) * BS : (block + offset + 1) * BS
            ]
            pieces.append(piece.reshape(BS * BS, query_local))
    pairs = jnp.stack(pieces)
    aux_blocks = lax.axis_size("blk") * PBD
    tiles = lax.all_gather(a_tiles, "grp", axis=0, tiled=True)
    codes = lax.all_gather(tile_codes, "grp", axis=0, tiled=True)
    count = tiles.shape[0]
    valid = codes >= 0
    pair = jnp.where(valid, codes % pair_count, 0).astype(jnp.int32)
    pblock = jnp.where(valid, codes // pair_count, -1).astype(jnp.int32)
    chosen = jnp.take(pairs, pair, axis=0)
    contrib = jnp.einsum("tik,tkq->tiq", tiles, chosen, preferred_element_type=jnp.float32)
    selector = (jnp.arange(aux_blocks, dtype=jnp.int32)[:, None] == pblock[None, :]).astype(
        jnp.float32
    )
    partial_chi = jnp.dot(
        selector, contrib.reshape(count, PB * query_local), precision=lax.Precision.HIGHEST
    )
    partial_chi = partial_chi.reshape(aux_blocks * PB, query_local)
    return lax.psum_scatter(partial_chi, "blk", scatter_dimension=0, tiled=True)


def solution(mesh):
    in_specs = (
        P("blk", None, None, "grp"),
        P("blk", "grp"),
        P(None, "grp"),
        P(),
        P(("blk", "grp"), None, None),
        P(("blk", "grp")),
    )
    out_specs = P("blk", "grp")
    return jax.shard_map(local, mesh=mesh, in_specs=in_specs, out_specs=out_specs, check_vma=False)
```

profile of v0, /device:TPU:0, one launch (start us, length us, event | category | flops | bytes accessed | tf_op | source)
XLA Modules:
  0.0 637.9 jit_solution(16914202088193835434)
XLA Ops:
  6.6 0.7 all-gather.3.cloned.1.call-update
  7.3 0.7 all-gather.5.cloned.1.call-update
  8.2 0.6 dynamic-slice
  9.7 10.6 %all-reduce = s32[32]{0:T(128)S(1)} all-reduce(s32[32]{0:T(128)S(1)} %dynamic-update-slice), channel_id=1, replica_groups=mesh['blk'=4,'grp'=8] {'grp'}, use_global_device_ids=true, to_apply=%add | all-reduce | flops 32 | bytes 256
  21.4 0.7 dynamic-slice_convert_fusion
  22.4 13.9 %all_gather.16 = bf16[96,384]{0,1:T(8,128)(2,1)S(1)} all-gather(bf16[96,48]{0,1:T(8,128)(2,1)S(1)} %copy-done.1), channel_id=1, replica_groups=mesh['blk'=4,'grp'=8] {'grp'}, dimensions={1}, use_global_device_ids=true | all-gather | bytes 82944 | tf_op jit(solution)/shard_map/all_gather | solution.py:16
  36.3 14.2 %all_gather.17 = bf16[384,384]{0,1:T(8,128)(2,1)S(1)} all-gather(bf16[384,48]{0,1:T(8,128)(2,1)S(1)} %copy-done), channel_id=1, replica_groups=mesh['blk'=4,'grp'=8] {'grp'}, dimensions={1}, use_global_device_ids=true | all-gather | bytes 331776 | tf_op jit(solution)/shard_map/all_gather | solution.py:17
  50.8 0.9 gather_fusion.1
  52.0 0.6 pad_clamp_fusion
  52.6 1.4 gather_fusion
  54.1 0.6 gather_fusion.2
  54.7 290.2 %all-gather.3.cloned.1.call-done = bf16[384,3,32,512]{3,2,1,0:T(8,128)(2,1)} async-done(((bf16[96,3,32,512]{3,2,1,0:T(8,128)(2,1)}), bf16[384,3,32,512]{3,2,1,0:T(8,128)(2,1)}) %all-gather.3.cloned.1.call-update) | async-done | bytes 37748752 | tf_op jit(solution)/shard_map/all_gather | solution.py:29
  344.8 36.7 %bitcast_convert_fusion = bf16[12,160,32,512]{3,1,2,0:T(8,128)(2,1)} fusion(bf16[12,32,3,32,512]{4,3,2,1,0:T(8,128)(2,1)} %bitcast.86, bf16[12,3,160,32]{2,3,1,0:T(8,128)(2,1)S(1)} %bitcast.73, pred[12,3]{1,0:T(8,128)(4,1)S(1)} %compare_and_fusion), kind=kOutput, calls=%fused_computation.4 | convolution fusion | flops 6071439360 | bytes 101031968 | tf_op jit(solution)/shard_map/wlds,ladsq->lawq/dot_general | solution.py:38
  381.5 56.2 %copy.44 = bf16[48,8,160,512]{3,1,2,0:T(8,128)(2,1)} copy(bf16[48,8,160,512]{3,2,1,0:T(8,128)(2,1)} %bitcast.71) | data formatting | bytes 125829120
  437.7 80.5 %copy.29 = bf16[81920,384]{1,0:T(8,128)(2,1)} copy(bf16[81920,384]{0,1:T(8,128)(2,1)} %bitcast.70) | data formatting | bytes 125829120 | tf_op jit(solution)/shard_map/dot_general | solution.py:40
  518.2 31.3 %convolution_convert_fusion = bf16[96,160,512]{2,0,1:T(8,128)(2,1)} fusion(bf16[160,512,384]{2,1,0:T(8,128)(2,1)} %bitcast.69, bf16[384,96]{1,0:T(8,128)(2,1)S(1)} %gather_fusion, pred[384]{0:T(512)(128)(4,1)S(1)} %iota_compare_fusion.2), kind=kOutput, calls=%fused_computation.9 | convolution fusion | flops 6047698944 | bytes 78717312 | tf_op jit(solution)/shard_map/dot_general | solution.py:40
  549.5 4.3 fusion.23
  559.1 1.1 bitcast_dynamic-update-slice_fusion.8
  560.1 1.1 bitcast_dynamic-update-slice_fusion.7
  561.2 1.0 bitcast_dynamic-update-slice_fusion.6
  562.2 1.1 bitcast_dynamic-update-slice_fusion.5
  563.3 1.0 bitcast_dynamic-update-slice_fusion.4
  564.4 1.0 bitcast_dynamic-update-slice_fusion.3
  565.4 1.1 bitcast_dynamic-update-slice_fusion.2
  566.5 1.1 bitcast_dynamic-update-slice_fusion.1
  567.5 1.0 bitcast_dynamic-update-slice_fusion
  568.6 16.7 %gather_fusion.3 = bf16[32,1024,512]{2,1,0:T(8,128)(2,1)} fusion(bf16[9,1024,512]{2,1,0:T(8,128)(2,1)} %bitcast_dynamic-update-slice_fusion, s32[1024]{0:T(1024)} %pad_clamp_fusion), kind=kCustom, calls=%fused_computation.3 | custom fusion | bytes 67108992 | tf_op jit(solution)/shard_map/jit(_take)/gather | solution.py:57
  585.3 14.7 %fusion = f32[32,512,32]{1,2,0:T(8,128)S(1)} fusion(bf16[32,32,1024]{2,1,0:T(8,128)(2,1)} %all-gather.5.cloned.1.call-done, bf16[32,1024,512]{2,1,0:T(8,128)(2,1)} %gather_fusion.3, pred[32]{0:T(512)(128)(4,1)S(1)} %copy-done.4), kind=kOutput, calls=%fused_computation.5 | convolution fusion | flops 1090519040 | bytes 37748768 | tf_op jit(solution)/shard_map/tik,tkq->tiq/dot_general | solution.py:58
  600.0 1.2 copy.45
  601.2 0.8 fusion.18
  602.1 1.2 reshape.142
  603.3 28.1 %reduce-scatter.2.cloned.1.call-done = f32[128,512]{1,0:T(8,128)} async-done(((f32[512,512]{1,0:T(8,128)}), f32[128,512]{1,0:T(8,128)}) %reduce-scatter.2.cloned.1.call-update) | async-done | bytes 262160 | tf_op jit(solution)/shard_map/reduce_scatter | solution.py:66
  (47 shorter events, 7.5 us)
Async XLA Ops:
  6.5 1.6 copy-start.5
  6.5 2.9 copy-start.3
  6.5 15.9 %copy-start.1 = (bf16[96,48]{0,1:T(8,128)(2,1)S(1)}, bf16[96,48]{0,1:T(8,128)(2,1)}, u32[]{:S(2)}) copy-start(bf16[96,48]{0,1:T(8,128)(2,1)} %param.7) | copy-start | bytes 27652
  6.5 29.8 %copy-start = (bf16[384,48]{0,1:T(8,128)(2,1)S(1)}, bf16[384,48]{0,1:T(8,128)(2,1)}, u32[]{:S(2)}) copy-start(bf16[384,48]{0,1:T(8,128)(2,1)} %param.8) | copy-start | bytes 110596
  6.5 338.3 %all-gather.3.cloned.1.call-start = ((), (), s32[]{:S(2)}) async-start(), calls=%async_computation.1 | async-start | bytes 47185920 | tf_op jit(solution)/shard_map/all_gather | solution.py:29
  7.3 578.1 %all-gather.5.cloned.1.call-start = ((), (), s32[]{:S(2)}) async-start(), calls=%async_computation.2 | async-start | bytes 2359296 | tf_op jit(solution)/shard_map/all_gather | solution.py:51
  8.0 623.3 %reduce-scatter.2.cloned.1.call-start = ((), (), s32[]{:S(2)}) async-start(), calls=%async_computation.3 | async-start | bytes 1310720 | tf_op jit(solution)/shard_map/reduce_scatter | solution.py:66
  568.6 16.8 %copy-start.4 = (pred[32]{0:T(512)(128)(4,1)S(1)}, pred[32]{0:T(512)(128)(4,1)}, u32[]{:S(2)}) copy-start(pred[32]{0:T(512)(128)(4,1)} %get-tuple-element.5) | copy-start | bytes 100
  585.3 15.9 %copy-start.2 = (s32[32]{0:T(128)S(1)}, s32[32]{0:T(128)}, u32[]{:S(2)}) copy-start(s32[32]{0:T(128)} %compare_select_fusion.6) | copy-start | bytes 388
Sparse Core Ops, SparseCore 0:
  9.2 335.5 all-gather.2
  346.4 29.1 all-gather.4
  603.4 27.8 reduce-scatter.1
where the time goes:
time: 640 us; the launch traced here: 638 us
  waiting for transfers between devices  320 us (50%)
  local copies, waits for them, and re-layouts  179 us (28%)
  matrix products  83.5 us (13%)
  blocking collectives  38.8 us (6%)
  between operations  14 us (2%)
    all_gather x1, waiting for transfers between devices, local(): accumulate_piece = lax.all_gather(b3c, 'blk', axis=0, tiled=True)  290 us
    dot_general x1, local copies, waits for them, and re-layouts, local(): paired = jnp.dot(occ_cols, inner, preferred_element_type=jnp.float32)  80.5 us
    unnamed x25, local copies, waits for them, and re-layouts  66.7 us
    dot_general x1, matrix products, local(): jnp.einsum('wlds,ladsq->lawq', virt_sel, tensor, preferred_element_type=j...  36.7 us
    dot_general x1, matrix products, local(): paired = jnp.dot(occ_cols, inner, preferred_element_type=jnp.float32)  31.3 us
    reduce_scatter x1, waiting for transfers between devices, local(): return lax.psum_scatter(partial_chi, 'blk', scatter_dimension=0, tiled=True)  28.1 us
    gather x1, local copies, waits for them, and re-layouts, local(): chosen = jnp.take(pairs, pair, axis=0)  16.7 us
    dot_general x1, matrix products, local(): jnp.einsum('tik,tkq->tiq', tiles, chosen, preferred_element_type=jnp.floa...  14.7 us
  transfers between devices with their start and end apart: 3, of which 2 were waited for; matrix products, arithmetic and copies ran while one was open for 39% of the time, Pallas kernels for 0%

commit v1 on v0

v1 whole, which is shorter than its diff:
```python
import functools

import jax
import jax.numpy as jnp
from jax import lax
from jax.experimental import pallas as pl
from jax.experimental.pallas import tpu as pltpu
from jax.sharding import PartitionSpec as P

BS = 32
PB = 32
KB = 3
BAND = 3
PBD = 4
LANES = 128
PACK = 4


def transform_kernel(nu_blocks, gv_ref, go_ref, b_ref, out_ref, *scratch):
    part = pl.program_id(1)
    rows, cols = gv_ref.shape[1], b_ref.shape[2]
    lam = b_ref.shape[0]
    for block in range(lam // BS):

        def first(i, carry):
            at = block * BS + i
            r = jnp.dot(gv_ref[block], b_ref[at], preferred_element_type=jnp.float32)
            for c, s in enumerate(scratch):
                s[pl.ds(at, rows, stride=lam), :] = r[:, c * LANES : (c + 1) * LANES]
            return carry

        lax.fori_loop(0, BS, first, 0)
    for nb in range(nu_blocks):
        start = pl.multiple_of((part * nu_blocks + nb) * BS, BS)
        occ = go_ref[pl.ds(start, BAND * BS), :]

        def second(i, carry):
            at = pl.multiple_of((nb * BS + i) * lam, lam)
            w = jnp.concatenate([s[pl.ds(at, lam), :] for s in scratch], axis=1)
            r = jnp.dot(occ, w.astype(jnp.bfloat16), preferred_element_type=jnp.float32)
            r = r.astype(jnp.bfloat16)
            to = pl.multiple_of(i * BS, BS)
            for j in range(BAND):
                out_ref[nb, BAND - 1 - j, pl.ds(to, BS), :] = r[j * BS : (j + 1) * BS]
            return carry

        lax.fori_loop(0, BS, second, 0)


def transform(b, gv, go):
    lam, band, q = b.shape
    nb_total = gv.shape[1] // BS
    cols = min(2 * LANES, q)
    nu_blocks = 6
    parts = nb_total // nu_blocks
    rows = nu_blocks * BS
    return pl.pallas_call(
        functools.partial(transform_kernel, nu_blocks),
        grid=(q // cols, parts),
        in_specs=[
            pl.BlockSpec((lam // BS, rows, band), lambda i, j: (0, j, 0)),
            pl.BlockSpec(go.shape, lambda i, j: (0, 0)),
            pl.BlockSpec((lam, band, cols), lambda i, j: (0, 0, i)),
        ],
        out_specs=pl.BlockSpec((nu_blocks, BAND, BS * BS, cols), lambda i, j: (j, 0, 0, i)),
        out_shape=jax.ShapeDtypeStruct((nb_total, BAND, BS * BS, q), jnp.bfloat16),
        scratch_shapes=[pltpu.VMEM((rows * lam, LANES), jnp.float32)] * (cols // LANES),
        compiler_params=pltpu.CompilerParams(vmem_limit_bytes=60 * 2**20),
        cost_estimate=pl.CostEstimate(
            flops=4 * lam * band * nb_total * BS * q, bytes_accessed=100 * 2**20, transcendentals=0
        ),
        name="transform",
    )(gv, go, b)


def tiles_kernel(pair_ref, slot_ref, row_ref, count_ref, *refs):
    tiles, (paired_ref, out_ref, acc) = refs[:PACK], refs[PACK:]
    step = pl.program_id(0)

    @pl.when(step == 0)
    def _():
        acc[...] = jnp.zeros_like(acc)

    @pl.when(step < count_ref[0])
    def _():
        lhs = jnp.concatenate([t[0] for t in tiles], axis=0)
        r = jnp.dot(lhs, paired_ref[0], preferred_element_type=jnp.float32)
        for t in range(PACK):
            at = row_ref[step * PACK + t]
            acc[at] += r[t * PB : (t + 1) * PB]

    @pl.when(step == pl.num_programs(0) - 1)
    def _():
        out_ref[...] = acc[: out_ref.shape[0]]


def contract(tiles, paired, pairs, slots, rows, count, aux):
    q = paired.shape[2]
    items = pairs.shape[0]

    def tile_spec(t):
        return pl.BlockSpec(
            (1, PB, BS * BS), lambda s, pair, slot, row, n: (slot[s * PACK + t], 0, 0)
        )

    return pl.pallas_call(
        tiles_kernel,
        grid_spec=pltpu.PrefetchScalarGridSpec(
            num_scalar_prefetch=4,
            grid=(items,),
            in_specs=[tile_spec(t) for t in range(PACK)]
            + [pl.BlockSpec((1, BS * BS, q), lambda s, pair, slot, row, n: (pair[s], 0, 0))],
            out_specs=pl.BlockSpec((aux, PB, q), lambda s, pair, slot, row, n: (0, 0, 0)),
            scratch_shapes=[pltpu.VMEM((aux + 1, PB, q), jnp.float32)],
        ),
        out_shape=jax.ShapeDtypeStruct((aux, PB, q), jnp.float32),
        compiler_params=pltpu.CompilerParams(vmem_limit_bytes=60 * 2**20),
        name="contract",
    )(pairs, slots, rows, count, *([tiles] * PACK), paired)


def schedule(pblock, pair, live, pair_total, aux):
    total = pair.shape[0]
    items = pair_total + total // PACK
    key = jnp.where(live, pair, pair_total)
    at = jnp.arange(total, dtype=jnp.int32)
    same = (key[:, None] == key[None, :]) & (at[None, :] < at[:, None])
    rank = jnp.sum(same, axis=1, dtype=jnp.int32)
    names = jnp.arange(pair_total, dtype=jnp.int32)
    number = jnp.sum(key[None, :] == names[:, None], axis=1, dtype=jnp.int32)
    groups = (number + PACK - 1) // PACK
    base = jnp.sum(jnp.where(names[None, :] < key[:, None], groups[None, :], 0), axis=1)
    place = jnp.where(live, (base + rank // PACK) * PACK + rank % PACK, -1)
    count = jnp.sum(groups, dtype=jnp.int32)
    hit = place[None, :] == jnp.arange(items * PACK, dtype=jnp.int32)[:, None]
    slots = jnp.sum(jnp.where(hit, at[None, :], 0), axis=1)
    rows = jnp.sum(jnp.where(hit, pblock[None, :] - aux, 0), axis=1) + aux
    start = jnp.cumsum(groups) - groups
    step = jnp.minimum(jnp.arange(items, dtype=jnp.int32), count - 1)
    pairs = jnp.max(
        jnp.where((start[None, :] <= step[:, None]) & (groups[None, :] > 0), names[None, :], 0),
        axis=1,
    )
    return pairs.astype(jnp.int32), slots.astype(jnp.int32), rows.astype(jnp.int32), count[None]


def local(b3c, green_occ, green_virt, occ_mask, a_tiles, tile_codes):
    n_blk, n_grp = lax.axis_size("blk"), lax.axis_size("grp")
    group = lax.axis_index("blk")
    lam, _, _, q = b3c.shape
    basis = green_virt.shape[0]
    blocks = basis // BS
    aux = n_blk * PBD
    slots_here = a_tiles.shape[0]

    turned = a_tiles.reshape(slots_here, PB, BS, BS).swapaxes(2, 3).reshape(a_tiles.shape)
    tiles = lax.all_gather(turned, ("blk", "grp"), axis=0, tiled=True)

    wide = green_occ.shape[1]
    quarter = lax.dynamic_slice_in_dim(green_virt, group * lam, lam, 0)
    pblock = jnp.where(tile_codes >= 0, tile_codes // (KB * BAND), -1)
    within = jnp.where(tile_codes >= 0, tile_codes % (KB * BAND), 0)
    coded = jnp.stack([pblock, within]).astype(jnp.bfloat16)
    coded = jnp.pad(coded, ((0, 14), (0, wide - slots_here)))
    sent = jnp.concatenate([green_occ, quarter, coded], axis=0)
    got = lax.all_gather(sent, ("blk", "grp"), axis=0, tiled=False)
    got = got.reshape(n_blk, n_grp, 2 * lam + 16, wide)
    whole = got[:, :, : 2 * lam].transpose(0, 2, 1, 3).reshape(n_blk, 2, lam, basis)
    occ_all = whole[:, 0].reshape(basis, basis)
    virt_all = whole[:, 1].reshape(basis, basis)
    codes = got[:, :, 2 * lam : 2 * lam + 2, :slots_here].astype(jnp.int32)
    pblock = codes[:, :, 0].reshape(-1)
    within = codes[:, :, 1].reshape(-1)

    mask = lax.dynamic_slice_in_dim(occ_mask, group * KB, KB, 1)
    mask = jnp.repeat(jnp.repeat(mask, BS, axis=0), BS, axis=1).astype(jnp.bfloat16)
    occ = lax.dynamic_slice_in_dim(occ_all, group * lam, lam, 1) * mask
    occ = jnp.concatenate([occ[-(BAND - 1) * BS :], occ], axis=0)
    virt = jnp.concatenate([virt_all, virt_all[:, : (BAND - 1) * BS]], axis=1)
    virt = lax.dynamic_slice_in_dim(virt, group * lam, lam + (BAND - 1) * BS, 1)
    virt = jnp.stack([virt[:, l * BS : (l + BAND) * BS] for l in range(KB)])

    paired = transform(b3c.reshape(lam, BAND * BS, q), virt, occ)
    paired = paired.reshape(blocks * BAND, BS * BS, q)

    owner = jnp.arange(pblock.shape[0], dtype=jnp.int32) // (n_grp * slots_here)
    offset = within % BAND
    nu = (owner * KB + within // BAND + offset) % blocks
    pairs, slots, rows, count = schedule(
        pblock, nu * BAND + offset, pblock >= 0, blocks * BAND, aux
    )
    chi = contract(tiles, paired, pairs, slots, rows, count, aux)
    chi = chi.reshape(n_blk, PBD * PB, q)

    total = lax.dynamic_index_in_dim(chi, group, 0, False)
    for d in range(1, n_blk):
        piece = lax.dynamic_index_in_dim(chi, (group + d) % n_blk, 0, False)
        moved = lax.ppermute(
            piece.astype(jnp.bfloat16), "blk", [(i, (i + d) % n_blk) for i in range(n_blk)]
        )
        total = total + moved.astype(jnp.float32)
    return total


def solution(mesh):
    in_specs = (
        P("blk", None, None, "grp"),
        P("blk", "grp"),
        P(None, "grp"),
        P(),
        P(("blk", "grp"), None, None),
        P(("blk", "grp")),
    )
    out_specs = P("blk", "grp")
    return jax.shard_map(local, mesh=mesh, in_specs=in_specs, out_specs=out_specs, check_vma=False)
```

time: 640 us -> 369 us (0.58)
  waiting for transfers between devices: 320 us -> 5.78 us
  Pallas kernels: 0 us -> 274 us
  local copies, waits for them, and re-layouts: 179 us -> 9.55 us
  matrix products: 83.5 us -> 0 us
  blocking collectives: 38.8 us -> 50.1 us
  other arithmetic: 2.51 us -> 11.3 us
    all_gather x2 -> x1, waiting for transfers between devices: 290 us -> 0.01 us  [local(): tiles = lax.all_gather(turned, ('blk', 'grp'), axis=0, tiled=True)]
    pallas_call x0 -> x2, Pallas kernels: none -> 274 us  [the longest x1 239 us: transform(): pl.pallas_call(functools.partial(transform_kernel, nu_blocks), grid=(q //...]
    dot_general x4 -> x0, matrix products: 83.5 us -> none  [the longest x1 36.7 us: local(): jnp.einsum('wlds,ladsq->lawq', virt_sel, tensor, preferred_element_type=j...]
    dot_general x1 -> x0, local copies, waits for them, and re-layouts: 80.5 us -> none  [local(): paired = jnp.dot(occ_cols, inner, preferred_element_type=jnp.float32)]
    unnamed x25 -> x6, local copies, waits for them, and re-layouts: 66.7 us -> 0.21 us
    reduce_scatter x1 -> x0, waiting for transfers between devices: 28.1 us -> none  [local(): return lax.psum_scatter(partial_chi, 'blk', scatter_dimension=0, tiled=True)]
    all_gather x2 -> x1, blocking collectives: 28.2 us -> 50.1 us  [local(): got = lax.all_gather(sent, ('blk', 'grp'), axis=0, tiled=False)]
    gather x5 -> x0, local copies, waits for them, and re-layouts: 19.9 us -> none  [the longest x1 16.7 us: local(): chosen = jnp.take(pairs, pair, axis=0)]
  transfers between devices with their start and end apart: 3 -> 4, of which waited for: 2 -> 2; matrix products, arithmetic and copies ran while one was open for 39% -> 4% of each run, Pallas kernels for 0% -> 65%
where the time goes in v1:
time: 369 us; the launch traced here: 368 us
  Pallas kernels  274 us (74%)
  blocking collectives  50.1 us (14%)
  between operations  14.2 us (4%)
  other arithmetic  11.3 us (3%)
  local copies, waits for them, and re-layouts  9.55 us (3%)
  waiting for transfers between devices  5.78 us (2%)
    pallas_call x1, Pallas kernels, transform(): pl.pallas_call(functools.partial(transform_kernel, nu_blocks), grid=(q //...  239 us
    all_gather x1, blocking collectives, local(): got = lax.all_gather(sent, ('blk', 'grp'), axis=0, tiled=False)  50.1 us
    pallas_call x1, Pallas kernels, contract(): pl.pallas_call(tiles_kernel, grid_spec=pltpu.PrefetchScalarGridSpec(num_s...  34.7 us
  transfers between devices with their start and end apart: 4, of which 2 were waited for; matrix products, arithmetic and copies ran while one was open for 4% of the time, Pallas kernels for 65%

profile of v1, /device:TPU:0, one launch (start us, length us, event | category | flops | bytes accessed | tf_op | source)
XLA Modules:
  0.0 368.0 jit_solution(4698891597409689228)
XLA Ops:
  6.5 1.9 reshape.294
  8.4 0.6 copy.34
  9.0 1.9 reshape.295
  11.0 0.7 convert_bitcast_fusion.1
  11.9 0.8 fusion.10
  12.7 50.1 %all-gather.1 = bf16[32,208,48]{1,2,0:T(8,128)(2,1)S(1)} all-gather(bf16[1,208,48]{1,2,0:T(8,128)(2,1)S(1)} %fusion.10), channel_id=2, replica_groups=mesh['blk'=4,'grp'=8] {'blk','grp'}, dimensions={0}, use_global_device_ids=true | all-gather | bytes 658944 | tf_op jit(solution)/shard_map/all_gather | solution.py:166
  62.8 0.4 reshape.296
  63.2 1.1 fusion.19
  64.3 0.5 copy.36
  65.2 0.1 copy.38
  65.5 0.5 copy.35
  66.1 1.7 add_reduce_fusion
  68.1 1.3 fusion.7
  69.4 0.1 ge.29
  69.5 0.1 ne.221
  70.0 0.1 reduce.4
  70.2 0.6 fusion.20
  71.5 0.2 convert_reduce_fusion
  71.7 0.7 pad_maximum_fusion.1.go_ref
  72.3 0.7 select_reduce_fusion.3.pair_ref
  73.0 0.2 fusion.2
  73.2 0.8 select_reduce_fusion
  74.0 0.1 slice_bitcast_fusion.3
  74.1 0.8 pad_maximum_fusion.gv_ref
  74.9 0.6 broadcast_add_fusion.row_ref
  75.5 239.3 %transform.1 = bf16[12,3,1024,512]{3,2,1,0:T(8,128)(2,1)} custom-call(bf16[3,384,96]{2,1,0:T(8,128)(2,1)} %pad_maximum_fusion.gv_ref, bf16[448,96]{1,0:T(8,128)(2,1)} %pad_maximum_fusion.1.go_ref, bf16[96,96,512]{2,1,0:T(8,128)(2,1)} %bitcast.52), custom_call_target="tpu_custom_call" | custom-call | flops 7247757312 | bytes 104857600 | tf_op jit(solution)/shard_map/transform/pallas_call | solution.py:57
  314.8 34.7 %contract.1 = f32[16,32,512]{2,1,0:T(8,128)} custom-call(s32[68]{0:T(128)} %select_reduce_fusion.3.pair_ref, s32[272]{0:T(512)} %get-tuple-element.11.slot_ref, s32[272]{0:T(512)} %broadcast_add_fusion.row_ref, s32[1]{0:T(128)} %bitcast.5.count_ref, bf16[128,32,1024]{2,1,0:T(8,128)(2,1)} %all-gather.4.cloned.1.call-done.refs_0_.refs_1_.refs_2_.refs_3_, ...), custom_call_target="tpu_custom_call" | custom-call | tf_op jit(solution)/shard_map/contract/pallas_call | solution.py:106
  349.5 1.2 fusion.3
  350.8 2.8 collective-permute-start.2
  353.6 4.4 %collective-permute-done = bf16[128,512]{1,0:T(8,128)(2,1)S(1)} collective-permute-done((bf16[128,512]{1,0:T(8,128)(2,1)S(1)}, bf16[128,512]{1,0:T(8,128)(2,1)S(1)}, u32[]{:S(2)}, u32[]{:S(2)}) %collective-permute-start) | collective-permute-done | bytes 131104 | tf_op jit(solution)/shard_map/ppermute | solution.py:198
  358.0 1.4 collective-permute-done.1
  359.4 1.7 fusion.1
  (36 shorter events, 1.7 us)
Async XLA Ops:
  6.5 5.3 %copy-start = (bf16[384,48]{0,1:T(8,128)(2,1)S(1)}, bf16[384,48]{0,1:T(8,128)(2,1)}, u32[]{:S(2)}) copy-start(bf16[384,48]{0,1:T(8,128)(2,1)} %param.8) | copy-start | bytes 110596
  6.5 58.3 %copy-start.1 = (s32[12,12]{1,0:T(8,128)S(1)}, s32[12,12]{1,0:T(8,128)}, u32[]{:S(2)}) copy-start(s32[12,12]{1,0:T(8,128)} %param.9) | copy-start | bytes 1732
  6.5 308.2 %all-gather.4.cloned.1.call-start = ((), (), s32[]{:S(2)}) async-start(), calls=%async_computation | async-start | bytes 8650752 | tf_op jit(solution)/shard_map/all_gather | solution.py:157
  350.6 7.4 %collective-permute-start = (bf16[128,512]{1,0:T(8,128)(2,1)S(1)}, bf16[128,512]{1,0:T(8,128)(2,1)S(1)}, u32[]{:S(2)}, u32[]{:S(2)}) collective-permute-start(bf16[128,512]{1,0:T(8,128)(2,1)S(1)} %get-tuple-element.14), channel_id=1, source_target_pairs={{0,8},{8,16},{16,24},{24,0},{1,9},{9,17},{17,25},{25,1},{2,10},{10... | collective-permute-start | bytes 393224 | tf_op jit(solution)/shard_map/ppermute | solution.py:198
  350.7 8.7 %collective-permute-start.1 = (bf16[128,512]{1,0:T(8,128)(2,1)S(1)}, bf16[128,512]{1,0:T(8,128)(2,1)S(1)}, u32[]{:S(2)}, u32[]{:S(2)}) collective-permute-start(bf16[128,512]{1,0:T(8,128)(2,1)S(1)} %get-tuple-element.16), channel_id=1, source_target_pairs={{0,16},{8,24},{16,0},{24,8},{1,17},{9,25},{17,1},{25,9},{2,18},{10... | collective-permute-start | bytes 393224 | tf_op jit(solution)/shard_map/ppermute | solution.py:198
  350.8 8.6 %collective-permute-start.2 = (bf16[128,512]{1,0:T(8,128)(2,1)S(1)}, bf16[128,512]{1,0:T(8,128)(2,1)S(1)}, u32[]{:S(2)}, u32[]{:S(2)}) collective-permute-start(bf16[128,512]{1,0:T(8,128)(2,1)S(1)} %get-tuple-element.15), channel_id=1, source_target_pairs={{0,24},{8,0},{16,8},{24,16},{1,25},{9,1},{17,9},{25,17},{2,26},{10... | collective-permute-start | bytes 393224 | tf_op jit(solution)/shard_map/ppermute | solution.py:198
Sparse Core Ops, SparseCore 0:
  11.1 81.3 all-gather.3
